TPU v7x, 32 devices: a whole 2x2x4 slice. The times are simulated.
32 devices in a mesh: dom: 16 (over z, x, core), vec: 2 (over y).
Axes of the slice: x: 2, y: 2, z: 4, core: 2. Of those that a mesh axis runs over, the one named last changes fastest.
Arguments:
- orbitals: bfloat16 [128, 65536], P(None, ('dom', 'vec'))
- projectors: bfloat16 [65536, 512], P('dom', 'vec'), may hold values from -0.0234375 to 0.0234375
- potential: float32 [65536], P(('dom', 'vec')), may hold values from 0 to 2
Outputs:
- filtered: bfloat16 [128, 65536], P(None, ('dom', 'vec'))
All inputs are finite; a program needn't handle non-finite values.
Results may differ from a plain program's by a relative error of at most 0.0052.
Values may be sent and summed in bfloat16 or wider, within the bound.
No kernel may reach another device: no remote copies, remote signals or barrier semaphores. Data moves between devices by JAX's collectives and lax.ppermute only.
A program may use at most 64 MiB of HBM per device.

v0:
```python
import jax
import jax.numpy as jnp
from jax import lax
from jax.sharding import PartitionSpec as P

CENTER = 1.0
HALF_WIDTH = 1.5
EPSILON = 1e-06


def hamiltonian(bands_now, projectors, shifted):
    partial_sum = jnp.dot(
        lax.all_gather(bands_now, "vec", axis=1, tiled=True),
        projectors,
        preferred_element_type=jnp.float32,
    )
    intersection_b = lax.psum(partial_sum, "dom").astype(jnp.bfloat16)
    action_terms = lax.dot_general(
        intersection_b, projectors, (((1,), (1,)), ((), ())), preferred_element_type=jnp.float32
    )
    actions = lax.psum_scatter(action_terms, "vec", scatter_dimension=1, tiled=True)
    return (shifted[None, :] * bands_now.astype(jnp.float32) - actions) / HALF_WIDTH


def chebyshev(bands_now, projectors, shifted):
    first_step = hamiltonian(bands_now, projectors, shifted).astype(jnp.bfloat16)
    return 2.0 * hamiltonian(first_step, projectors, shifted) - bands_now.astype(jnp.float32)


def body(orbitals, projectors, potential):
    local_rows = orbitals.shape[1]
    grid_count = local_rows * lax.axis_size("dom") * lax.axis_size("vec")
    shifted = potential - CENTER
    panel_list = [orbitals]
    seconds = [chebyshev(bands_now, projectors, shifted) for bands_now in panel_list]
    second = seconds[0]
    square_sum = lax.psum(jnp.sum(second * second, axis=1), ("dom", "vec"))
    normed_list = second * lax.rsqrt(square_sum / grid_count + EPSILON)[:, None]
    return normed_list.astype(jnp.bfloat16)


def solution(mesh):
    return jax.shard_map(
        body,
        mesh=mesh,
        in_specs=(P(None, ("dom", "vec")), P("dom", "vec"), P(("dom", "vec"))),
        out_specs=P(None, ("dom", "vec")),
        check_vma=False,
    )
```

profile of v0, /device:TPU:0, one launch (start us, length us, event | category | flops | bytes accessed | tf_op | source)
XLA Modules:
  0.0 294.5 jit_solution(7076762438744303975)
XLA Ops:
  6.5 0.0 copy-start
  6.5 0.0 all-gather.3.cloned.1.call-start
  6.5 0.7 all-gather.3.cloned.1.call-update
  7.3 0.0 reduce-scatter.3.cloned.1.call-start
  7.3 25.6 %all-gather.3.cloned.1.call-done = bf16[128,4096]{1,0:T(8,128)(2,1)} async-done(((bf16[128,2048]{1,0:T(8,128)(2,1)}), bf16[128,4096]{1,0:T(8,128)(2,1)}) %all-gather.3.cloned.1.call-update) | async-done | bytes 1048592 | tf_op jit(solution)/shard_map/all_gather | solution.py:13
  32.9 0.0 copy-done
  32.9 1.7 fusion.7
  34.6 61.8 %all-reduce.2 = bf16[128,256]{1,0:T(8,128)(2,1)S(1)} all-reduce(f32[128,256]{1,0:T(8,128)S(1)} %fusion.7), channel_id=1, replica_groups=mesh['dom'=16,'vec'=2] {'dom'}, use_global_device_ids=true, to_apply=%region_0.0 | all-reduce | flops 32768 | bytes 196608 | tf_op jit(solution)/shard_map/psum | solution.py:17
  96.4 2.2 fusion.10
  98.6 0.0 copy-start.3
  98.6 0.0 copy-start.1
  98.6 0.0 reduce-scatter.3.cloned.1.call-update
  98.6 0.0 all-gather.5.cloned.1.call-start
  98.7 0.6 copy-done.3
  99.3 27.8 %reduce-scatter.3.cloned.1.call-done = f32[128,2048]{1,0:T(8,128)} async-done(((f32[128,4096]{1,0:T(8,128)}), f32[128,2048]{1,0:T(8,128)}) %reduce-scatter.3.cloned.1.call-update) | async-done | bytes 1048592 | tf_op jit(solution)/shard_map/reduce_scatter | solution.py:21
  127.1 0.0 copy-done.1
  127.1 2.2 fusion.2
  129.2 0.0 all-gather.5.cloned.1.call-update
  129.3 0.0 reduce-scatter.5.cloned.1.call-start
  129.3 21.4 %all-gather.5.cloned.1.call-done = bf16[128,4096]{1,0:T(8,128)(2,1)} async-done(((bf16[128,2048]{1,0:T(8,128)(2,1)}), bf16[128,4096]{1,0:T(8,128)(2,1)}) %all-gather.5.cloned.1.call-update) | async-done | bytes 1048592 | tf_op jit(solution)/shard_map/all_gather | solution.py:13
  150.7 1.7 fusion.8
  152.4 61.8 %all-reduce.3 = bf16[128,256]{1,0:T(8,128)(2,1)S(1)} all-reduce(f32[128,256]{1,0:T(8,128)S(1)} %fusion.8), channel_id=1, replica_groups=mesh['dom'=16,'vec'=2] {'dom'}, use_global_device_ids=true, to_apply=%region_2.0 | all-reduce | flops 32768 | bytes 196608 | tf_op jit(solution)/shard_map/psum | solution.py:17
  214.2 2.2 fusion.9
  216.4 0.0 copy-start.2
  216.4 0.0 reduce-scatter.5.cloned.1.call-update
  216.4 28.4 %reduce-scatter.5.cloned.1.call-done = f32[128,2048]{1,0:T(8,128)} async-done(((f32[128,4096]{1,0:T(8,128)}), f32[128,2048]{1,0:T(8,128)}) %reduce-scatter.5.cloned.1.call-update) | async-done | bytes 1048592 | tf_op jit(solution)/shard_map/reduce_scatter | solution.py:21
  244.8 0.0 copy-done.2
  244.8 1.6 multiply_reduce_fusion
  246.4 39.3 %psum.23 = f32[128]{0:T(128)S(1)} all-reduce(f32[128]{0:T(128)S(1)} %multiply_reduce_fusion), channel_id=1, replica_groups=mesh['dom'=16,'vec'=2] {'dom','vec'}, use_global_device_ids=true, to_apply=%region_5.0 | all-reduce | flops 128 | bytes 1024 | tf_op jit(solution)/shard_map/psum | solution.py:37
  285.7 2.3 multiply_convert_fusion
  (2 shorter events, 0.0 us)
Async XLA Ops:
  6.5 26.4 %copy-start = (bf16[4096,256]{1,0:T(8,128)(2,1)S(1)}, bf16[4096,256]{1,0:T(8,128)(2,1)}, u32[]{:S(2)}) copy-start(bf16[4096,256]{1,0:T(8,128)(2,1)} %param.4) | copy-start | bytes 6291460
  6.5 26.4 %all-gather.3.cloned.1.call-start = ((), (), s32[]{:S(2)}) async-start(), calls=%async_computation.2 | async-start | bytes 1572864 | tf_op jit(solution)/shard_map/all_gather | solution.py:13
  7.3 119.8 %reduce-scatter.3.cloned.1.call-start = ((), (), s32[]{:S(2)}) async-start(), calls=%async_computation.3 | async-start | bytes 3145728 | tf_op jit(solution)/shard_map/reduce_scatter | solution.py:21
  98.6 0.7 copy-start.3
  98.6 28.5 %copy-start.1 = (bf16[128,2048]{1,0:T(8,128)(2,1)S(1)}, bf16[128,2048]{1,0:T(8,128)(2,1)}, u32[]{:S(2)}) copy-start(bf16[128,2048]{1,0:T(8,128)(2,1)} %param.3) | copy-start | bytes 1572868
  98.6 52.1 %all-gather.5.cloned.1.call-start = ((), (), s32[]{:S(2)}) async-start(), calls=%async_computation.4 | async-start | bytes 1572864 | tf_op jit(solution)/shard_map/all_gather | solution.py:13
  129.3 115.6 %reduce-scatter.5.cloned.1.call-start = ((), (), s32[]{:S(2)}) async-start(), calls=%async_computation.5 | async-start | bytes 3145728 | tf_op jit(solution)/shard_map/reduce_scatter | solution.py:21
  216.4 28.5 %copy-start.2 = (bf16[128,2048]{1,0:T(8,128)(2,1)S(1)}, bf16[128,2048]{1,0:T(8,128)(2,1)}, u32[]{:S(2)}) copy-start(bf16[128,2048]{1,0:T(8,128)(2,1)} %fusion.2) | copy-start | bytes 1572868
Sparse Core Ops, SparseCore 0:
  8.9 23.9 all-gather.2
  98.7 28.2 reduce-scatter.2
  129.4 21.2 all-gather.4
  216.5 28.2 reduce-scatter.4
where the time goes:
time: 295 us
  blocking collectives  163 us (55%)
  waiting for transfers between devices  104 us (35%)
  between operations  13.2 us (4%)
  matrix products  7.67 us (3%)
  other arithmetic  6.06 us (2%)
    psum x2, blocking collectives, hamiltonian(): intersection_b = lax.psum(partial_sum, 'dom').astype(jnp.bfloat16)  124 us
    reduce_scatter x2, waiting for transfers between devices, hamiltonian(): lax.psum_scatter(action_terms, 'vec', scatter_dimension=1, tiled=True)  56.2 us
    all_gather x2, waiting for transfers between devices, hamiltonian(): lax.all_gather(bands_now, 'vec', axis=1, tiled=True)  47 us
    psum x1, blocking collectives, body(): square_sum = lax.psum(jnp.sum(second * second, axis=1), ('dom', 'vec'))  39.3 us
  transfers between devices with their start and end apart: 4, of which 4 were waited for; matrix products, arithmetic and copies ran while one was open for 0% of the time, Pallas kernels for 0%

commit v1 on v0

--- a/solution.py
+++ b/solution.py
@@ -14,7 +14,7 @@
         projectors,
         preferred_element_type=jnp.float32,
     )
-    intersection_b = lax.psum(partial_sum, "dom").astype(jnp.bfloat16)
+    intersection_b = jnp.sum(lax.all_gather(partial_sum, "dom"), axis=0).astype(jnp.bfloat16)
     action_terms = lax.dot_general(
         intersection_b, projectors, (((1,), (1,)), ((), ())), preferred_element_type=jnp.float32
     )

time: 295 us -> 264 us (0.89)
  blocking collectives: 163 us -> 39.3 us
  waiting for transfers between devices: 104 us -> 192 us
  other arithmetic: 6.06 us -> 9.52 us
    psum x2 -> x0, blocking collectives: 124 us -> none  [hamiltonian(): intersection_b = lax.psum(partial_sum, 'dom').astype(jnp.bfloat16)]
    all_gather x0 -> x2, waiting for transfers between devices: none -> 83.1 us  [hamiltonian(): lax.all_gather(partial_sum, 'dom')]
    reduce_scatter x2, waiting for transfers between devices: 56.2 us -> 60.9 us  [hamiltonian(): lax.psum_scatter(action_terms, 'vec', scatter_dimension=1, tiled=True)]
    reduce_sum x0 -> x2, other arithmetic: none -> 3.46 us  [hamiltonian(): jnp.sum(lax.all_gather(partial_sum, 'dom'), axis=0).astype(jnp.bfloat16)]
  transfers between devices with their start and end apart: 4 -> 6, of which waited for: 4 -> 6; matrix products, arithmetic and copies ran while one was open for 0% -> 0% of each run, Pallas kernels for 0% -> 0%
where the time goes in v1:
time: 264 us
  waiting for transfers between devices  192 us (73%)
  blocking collectives  39.3 us (15%)
  between operations  13.5 us (5%)
  other arithmetic  9.52 us (4%)
  matrix products  8.93 us (3%)
    all_gather x2, waiting for transfers between devices, hamiltonian(): lax.all_gather(partial_sum, 'dom')  83.1 us
    reduce_scatter x2, waiting for transfers between devices, hamiltonian(): lax.psum_scatter(action_terms, 'vec', scatter_dimension=1, tiled=True)  60.9 us
    all_gather x2, waiting for transfers between devices, hamiltonian(): lax.all_gather(bands_now, 'vec', axis=1, tiled=True)  47 us
    psum x1, blocking collectives, body(): square_sum = lax.psum(jnp.sum(second * second, axis=1), ('dom', 'vec'))  39.3 us
  transfers between devices with their start and end apart: 6, of which 6 were waited for; matrix products, arithmetic and copies ran while one was open for 0% of the time, Pallas kernels for 0%

profile of v1, /device:TPU:0, one launch (start us, length us, event | category | flops | bytes accessed | tf_op | source)
XLA Modules:
  0.0 263.9 jit_solution(17864897146212749493)
XLA Ops:
  6.5 0.0 copy-start
  6.5 0.0 all-gather.7.cloned.1.call-start
  6.5 0.7 all-gather.7.cloned.1.call-update
  7.3 0.0 all-gather.11.cloned.1.call-start
  7.3 25.6 %all-gather.7.cloned.1.call-done = bf16[128,4096]{1,0:T(8,128)(2,1)} async-done(((bf16[128,2048]{1,0:T(8,128)(2,1)}), bf16[128,4096]{1,0:T(8,128)(2,1)}) %all-gather.7.cloned.1.call-update) | async-done | bytes 1048592 | tf_op jit(solution)/shard_map/all_gather | solution.py:13
  32.9 0.0 copy-done
  32.9 2.3 fusion.7
  35.2 0.0 all-gather.11.cloned.1.call-update
  35.3 0.0 reduce-scatter.3.cloned.1.call-start
  35.3 41.6 %all-gather.11.cloned.1.call-done = f32[2048,256]{1,0:T(8,128)} async-done(((f32[128,256]{1,0:T(8,128)}), f32[2048,256]{1,0:T(8,128)}) %all-gather.11.cloned.1.call-update) | async-done | bytes 2097168 | tf_op jit(solution)/shard_map/all_gather | solution.py:17
  76.9 1.7 reduce_sum.27
  78.6 2.1 fusion.10
  80.7 0.0 copy-start.3
  80.7 0.0 copy-start.1
  80.7 0.0 reduce-scatter.3.cloned.1.call-update
  80.8 0.0 all-gather.9.cloned.1.call-start
  80.8 0.6 copy-done.3
  81.4 30.1 %reduce-scatter.3.cloned.1.call-done = f32[128,2048]{1,0:T(8,128)} async-done(((f32[128,4096]{1,0:T(8,128)}), f32[128,2048]{1,0:T(8,128)}) %reduce-scatter.3.cloned.1.call-update) | async-done | bytes 1048592 | tf_op jit(solution)/shard_map/reduce_scatter | solution.py:21
  111.6 0.0 copy-done.1
  111.6 2.2 fusion.2
  113.8 0.0 all-gather.9.cloned.1.call-update
  113.8 0.0 all-gather.13.cloned.1.call-start
  113.8 21.4 %all-gather.9.cloned.1.call-done = bf16[128,4096]{1,0:T(8,128)(2,1)} async-done(((bf16[128,2048]{1,0:T(8,128)(2,1)}), bf16[128,4096]{1,0:T(8,128)(2,1)}) %all-gather.9.cloned.1.call-update) | async-done | bytes 1048592 | tf_op jit(solution)/shard_map/all_gather | solution.py:13
  135.2 2.3 fusion.8
  137.5 0.0 all-gather.13.cloned.1.call-update
  137.6 0.0 reduce-scatter.5.cloned.1.call-start
  137.6 41.6 %all-gather.13.cloned.1.call-done = f32[2048,256]{1,0:T(8,128)} async-done(((f32[128,256]{1,0:T(8,128)}), f32[2048,256]{1,0:T(8,128)}) %all-gather.13.cloned.1.call-update) | async-done | bytes 2097168 | tf_op jit(solution)/shard_map/all_gather | solution.py:17
  179.2 1.7 reduce_sum.28
  180.9 2.1 fusion.9
  183.0 0.0 copy-start.2
  183.0 0.0 reduce-scatter.5.cloned.1.call-update
  183.1 30.8 %reduce-scatter.5.cloned.1.call-done = f32[128,2048]{1,0:T(8,128)} async-done(((f32[128,4096]{1,0:T(8,128)}), f32[128,2048]{1,0:T(8,128)}) %reduce-scatter.5.cloned.1.call-update) | async-done | bytes 1048592 | tf_op jit(solution)/shard_map/reduce_scatter | solution.py:21
  213.8 0.0 copy-done.2
  213.8 1.6 multiply_reduce_fusion
  215.4 39.3 %psum.7 = f32[128]{0:T(128)S(1)} all-reduce(f32[128]{0:T(128)S(1)} %multiply_reduce_fusion), channel_id=1, replica_groups=mesh['dom'=16,'vec'=2] {'dom','vec'}, use_global_device_ids=true, to_apply=%region_5.0 | all-reduce | flops 128 | bytes 1024 | tf_op jit(solution)/shard_map/psum | solution.py:37
  254.7 2.3 multiply_convert_fusion
  (2 shorter events, 0.0 us)
Async XLA Ops:
  6.5 26.4 %copy-start = (bf16[4096,256]{1,0:T(8,128)(2,1)S(1)}, bf16[4096,256]{1,0:T(8,128)(2,1)}, u32[]{:S(2)}) copy-start(bf16[4096,256]{1,0:T(8,128)(2,1)} %param.4) | copy-start | bytes 6291460
  6.5 26.4 %all-gather.7.cloned.1.call-start = ((), (), s32[]{:S(2)}) async-start(), calls=%async_computation.2 | async-start | bytes 1572864 | tf_op jit(solution)/shard_map/all_gather | solution.py:13
  7.3 69.6 %all-gather.11.cloned.1.call-start = ((), (), s32[]{:S(2)}) async-start(), calls=%async_computation.6 | async-start | bytes 2228224 | tf_op jit(solution)/shard_map/all_gather | solution.py:17
  35.3 76.3 %reduce-scatter.3.cloned.1.call-start = ((), (), s32[]{:S(2)}) async-start(), calls=%async_computation.3 | async-start | bytes 3145728 | tf_op jit(solution)/shard_map/reduce_scatter | solution.py:21
  80.7 0.7 copy-start.3
  80.7 30.8 %copy-start.1 = (bf16[128,2048]{1,0:T(8,128)(2,1)S(1)}, bf16[128,2048]{1,0:T(8,128)(2,1)}, u32[]{:S(2)}) copy-start(bf16[128,2048]{1,0:T(8,128)(2,1)} %param.3) | copy-start | bytes 1572868
  80.8 54.4 %all-gather.9.cloned.1.call-start = ((), (), s32[]{:S(2)}) async-start(), calls=%async_computation.4 | async-start | bytes 1572864 | tf_op jit(solution)/shard_map/all_gather | solution.py:13
  113.8 65.4 %all-gather.13.cloned.1.call-start = ((), (), s32[]{:S(2)}) async-start(), calls=%async_computation.7 | async-start | bytes 2228224 | tf_op jit(solution)/shard_map/all_gather | solution.py:17
  137.6 76.3 %reduce-scatter.5.cloned.1.call-start = ((), (), s32[]{:S(2)}) async-start(), calls=%async_computation.5 | async-start | bytes 3145728 | tf_op jit(solution)/shard_map/reduce_scatter | solution.py:21
  183.0 30.8 %copy-start.2 = (bf16[128,2048]{1,0:T(8,128)(2,1)S(1)}, bf16[128,2048]{1,0:T(8,128)(2,1)}, u32[]{:S(2)}) copy-start(bf16[128,2048]{1,0:T(8,128)(2,1)} %fusion.2) | copy-start | bytes 1572868
Sparse Core Ops, SparseCore 0:
  8.9 23.9 all-gather.6
  35.4 41.4 all-gather.10
  80.9 30.6 reduce-scatter.2
  113.9 21.2 all-gather.8
  137.7 41.4 all-gather.12
  183.2 30.6 reduce-scatter.4
